TPU v7x, 128 devices: a whole 4x4x4 slice. The times are simulated.
128 devices in a mesh: tenant: 32 (over z, x, y_lo), tp: 4 (over y_hi, core).
Axes of the slice: x: 4, y: 4 (y_hi: 2, y_lo: 2; y = y_hi * 2 + y_lo), z: 4, core: 2. Of those that a mesh axis runs over, the one named last changes fastest.
Arguments:
- src_tokens: bfloat16 [1536, 64, 1024], P('tenant'), may hold values from -64 to 64
- pair_tenant: int32 [1536], P('tenant'), may hold values from 0 to 31, as said below
- pair_length: int32 [1536], P('tenant'), may hold values from 1 to 64
- norm_gain: float32 [32, 1024], P('tenant'), may hold values from 0.1 to 1.9
- w_query: bfloat16 [32, 1024, 4096], P('tenant', None, 'tp'), may hold values from -1 to 1
- w_key: bfloat16 [32, 1024, 4096], P('tenant', None, 'tp'), may hold values from -1 to 1
- w_value: bfloat16 [32, 1024, 4096], P('tenant', None, 'tp'), may hold values from -0.1875 to 0.1875
- w_out: bfloat16 [32, 4096, 1024], P('tenant', 'tp'), may hold values from -0.09375 to 0.09375
- rel_bias: float32 [32, 32, 32], P('tenant', None, 'tp'), may hold values from -6 to 6
Outputs:
- layer_out: bfloat16 [65536, 1024], P(('tenant', 'tp'))
Inputs may be any that keep to these rules, and one draw needn't show every extreme that they name: `pair_tenant`: the pairs of one retriever shard bound for one tenant have pair_length summing to at most 64; in every draw some tenant receives exactly 64 tokens from every shard.
All inputs are finite; a program needn't handle non-finite values.
Results may differ from a plain program's by a relative error of at most 0.0065.
Values may be sent and summed in bfloat16 or wider, within the bound.
A program may use at most 128 MiB of HBM per device.

v0:
```python
import math
import jax
import jax.numpy as jnp
import numpy as np
from jax import lax
from jax.sharding import PartitionSpec as P


def in_blocks(value, dim, length):
    before, after = (value.shape[:dim], value.shape[dim + 1 :])
    return jnp.moveaxis(value.reshape(*before, length, -1, *after), dim, 0)


def summed_on_arrival(value, axis, dim):
    length = lax.axis_size(axis)
    pieces = lax.all_to_all(in_blocks(value, dim, length), axis, 0, 0, tiled=True)
    return jnp.sum(pieces.astype(jnp.float32), axis=0)


def bucket_grid(extent, buckets):
    offsets = np.arange(extent)[None, :] - np.arange(extent)[:, None]
    half_count = buckets // 2
    upward = np.where(offsets > 0, half_count, 0)
    distance = np.abs(offsets)
    exact_limit = half_count // 2
    ratio = np.maximum(distance, 1) / exact_limit
    spread_bucket = exact_limit + np.floor(
        np.log(ratio) / math.log(128.0 / exact_limit) * (half_count - exact_limit)
    ).astype(np.int32)
    spread_bucket = np.minimum(spread_bucket, half_count - 1)
    return (upward + np.where(distance < exact_limit, distance, spread_bucket)).astype(np.int32)


def rms_normed(tenant_rows, gain_row):
    values = tenant_rows.astype(jnp.float32)
    mean_square = jnp.mean(values * values, axis=-1, keepdims=True)
    return (values * lax.rsqrt(mean_square + 1e-06) * gain_row).astype(jnp.bfloat16)


def pack_rows(tokens, tenant, length, first_id, tenants):
    shard_pairs, slot_rows, feature_count = tokens.shape
    pair_order = jnp.arange(shard_pairs, dtype=jnp.int32)
    earlier = (tenant[:, None] == tenant[None, :]) & (pair_order[None, :] < pair_order[:, None])
    offset = jnp.sum(jnp.where(earlier, length[None, :], 0), axis=1)
    position = jnp.arange(slot_rows, dtype=jnp.int32)
    target = (tenant * slot_rows + offset)[:, None] + position[None, :]
    target = jnp.where(position[None, :] < length[:, None], target, tenants * slot_rows)
    flat_target = target.reshape(-1)
    packed = (
        jnp.zeros((tenants * slot_rows, feature_count), tokens.dtype)
        .at[flat_target]
        .set(tokens.reshape(-1, feature_count), mode="drop")
    )
    pair_ids = jnp.broadcast_to((first_id + pair_order)[:, None], target.shape).reshape(-1)
    segment = (
        jnp.full((tenants * slot_rows,), -1, jnp.int32).at[flat_target].set(pair_ids, mode="drop")
    )
    return (packed.reshape(tenants, slot_rows, feature_count), segment.reshape(tenants, slot_rows))


def attend(normed, segment, query_weight, key_weight, value_weight, bias_table, slot_rows, tenants):
    row_total = normed.shape[0]
    local_heads = bias_table.shape[1]
    head_size = query_weight.shape[1] // local_heads
    query_rows = jnp.dot(normed, query_weight, preferred_element_type=jnp.float32).astype(
        jnp.bfloat16
    )
    key_rows = jnp.dot(normed, key_weight, preferred_element_type=jnp.float32).astype(jnp.bfloat16)
    value_rows = jnp.dot(normed, value_weight, preferred_element_type=jnp.float32).astype(
        jnp.bfloat16
    )
    block_rows = slot_rows * min(max(1, 128 // slot_rows), tenants)
    block_count = row_total // block_rows
    bucket_index = jnp.asarray(bucket_grid(block_rows, bias_table.shape[0]))
    bucket_match = (
        bucket_index[:, :, None] == jnp.arange(bias_table.shape[0], dtype=jnp.int32)[None, None, :]
    ).astype(jnp.float32)
    position_bias = jnp.einsum(
        "qkb,bh->hqk", bucket_match, bias_table, precision=lax.Precision.HIGHEST
    )
    query_blocks = query_rows.reshape(block_count, block_rows, local_heads, head_size)
    key_blocks = key_rows.reshape(block_count, block_rows, local_heads, head_size)
    value_blocks = value_rows.reshape(block_count, block_rows, local_heads, head_size)
    scores = jnp.einsum(
        "bqhd,bkhd->bhqk", query_blocks, key_blocks, preferred_element_type=jnp.float32
    )
    scores = scores + position_bias[None]
    segment_blocks = segment.reshape(block_count, block_rows)
    allowed = (segment_blocks[:, :, None] == segment_blocks[:, None, :]) & (
        segment_blocks[:, None, :] >= 0
    )
    scores = jnp.where(allowed[:, None], scores, -1000000000.0)
    maxima = jnp.max(scores, axis=-1, keepdims=True)
    weights = jnp.exp(scores - maxima)
    probabilities = (weights / jnp.sum(weights, axis=-1, keepdims=True)).astype(jnp.bfloat16)
    context = jnp.einsum(
        "bhqk,bkhd->bqhd", probabilities, value_blocks, preferred_element_type=jnp.float32
    )
    return context.astype(jnp.bfloat16).reshape(row_total, local_heads * head_size)


def per_device(
    src_tokens, pair_tenant, pair_length, norm_gain, w_query, w_key, w_value, w_out, rel_bias
):
    tenants = lax.axis_size("tenant")
    shard_pairs, slot_rows, feature_count = src_tokens.shape
    first_id = lax.axis_index("tenant") * shard_pairs
    column_share = feature_count // lax.axis_size("tp")
    columns = lax.dynamic_slice_in_dim(
        src_tokens, lax.axis_index("tp") * column_share, column_share, 2
    )
    packed, segment = pack_rows(columns, pair_tenant, pair_length, first_id, tenants)
    arrived, arrived_segment = (
        lax.all_to_all(packed, "tenant", split_axis=0, concat_axis=0, tiled=True),
        lax.all_to_all(segment, "tenant", split_axis=0, concat_axis=0, tiled=True),
    )
    arrived = lax.all_gather(
        arrived.reshape(tenants * slot_rows, column_share), "tp", axis=1, tiled=True
    )
    arrived_segment = arrived_segment.reshape(-1)
    normed = rms_normed(arrived, norm_gain[0])
    context = attend(
        normed, arrived_segment, w_query[0], w_key[0], w_value[0], rel_bias[0], slot_rows, tenants
    )
    out_weight = w_out[0]
    row_total = arrived.shape[0]
    own_rows = row_total // lax.axis_size("tp")
    head_total = summed_on_arrival(
        jnp.dot(context, out_weight, preferred_element_type=jnp.float32).astype(jnp.bfloat16),
        "tp",
        0,
    )
    first_row = lax.axis_index("tp") * own_rows
    residual = lax.dynamic_slice_in_dim(arrived, first_row, own_rows, 0).astype(jnp.float32)
    occupied = lax.dynamic_slice_in_dim(arrived_segment, first_row, own_rows, 0) >= 0
    return jnp.where(occupied[:, None], residual + head_total, 0.0).astype(jnp.bfloat16)


def solution(mesh):
    in_specs = (
        P("tenant", None, None),
        P("tenant"),
        P("tenant"),
        P("tenant", None),
        P("tenant", None, "tp"),
        P("tenant", None, "tp"),
        P("tenant", None, "tp"),
        P("tenant", "tp", None),
        P("tenant", None, "tp"),
    )
    out_specs = P(("tenant", "tp"), None)
    return jax.shard_map(
        per_device, mesh=mesh, in_specs=in_specs, out_specs=out_specs, check_vma=False
    )
```

profile of v0, /device:TPU:1, one launch (start us, length us, event | category | flops | bytes accessed | tf_op | source)
XLA Modules:
  0.0 213.1 jit_solution(8039649190054375029)
XLA Ops:
  6.6 1.0 select_reduce_fusion
  7.6 0.7 multiply_add_fusion
  8.2 0.7 add_select_fusion.4
  9.1 2.7 %constant_dynamic-slice_fusion = bf16[48,64,256]{2,1,0:T(8,128)(2,1)} fusion(bf16[48,64,1024]{2,1,0:T(8,128)(2,1)} %param.10, s32[]{:T(128)S(6)} %select_n.50), kind=kLoop, calls=%fused_computation.55 | loop fusion | bytes 3145732 | tf_op jit(solution)/shard_map/dynamic_slice | solution.py:109
  11.8 14.2 %scatter_custom_fusion.1 = bf16[2048,256]{1,0:T(8,128)(2,1)S(1)} fusion(s32[3072]{0:T(1024)S(1)} %bitcast.57, bf16[3072,256]{1,0:T(8,128)(2,1)} %bitcast.55, bf16[]{:T(256)} %constant.10.clone.1), kind=kCustom, calls=%fused_computation.40 | custom fusion | bytes 1049088 | tf_op jit(solution)/shard_map/scatter | solution.py:52
  26.0 26.3 %all_to_all.19 = bf16[32,64,256]{2,1,0:T(8,128)(2,1)} all-to-all(bf16[32,64,256]{2,1,0:T(8,128)(2,1)S(1)} %bitcast.54), channel_id=1, replica_groups=mesh['tenant'=32,'tp'=4] {'tenant'}, dimensions={0} | all-to-all | bytes 2097152 | tf_op jit(solution)/shard_map/all_to_all | solution.py:114
  52.5 11.8 %scatter_custom_fusion = s32[2048]{0:T(1024)S(1)} fusion(s32[3072]{0:T(1024)S(1)} %bitcast.58, s32[3072]{0:T(1024)S(1)} %reshape.140, s32[]{:T(128)} %constant.18.clone.1), kind=kCustom, calls=%fused_computation.51 | custom fusion | bytes 8196 | tf_op jit(solution)/shard_map/scatter | solution.py:56
  64.3 0.7 all_to_all.12
  65.0 4.0 %all-to-all-start = ((s32[32,1,64]{2,1,0:T(1,128)}), s32[32,1,64]{2,1,0:T(1,128)S(1)}, u32[]{:S(2)}, u32[]{:S(2)}) async-start(s32[32,1,64]{2,1,0:T(1,128)} %all_to_all.12), calls=%async_computation | async-start | bytes 32768 | tf_op jit(solution)/shard_map/all_to_all | solution.py:115
  69.1 0.7 fusion.27
  70.0 5.9 %all-to-all-done = s32[32,1,64]{2,1,0:T(1,128)S(1)} async-done(((s32[32,1,64]{2,1,0:T(1,128)}), s32[32,1,64]{2,1,0:T(1,128)S(1)}, u32[]{:S(2)}, u32[]{:S(2)}) %all-to-all-start) | async-done | bytes 8224 | tf_op jit(solution)/shard_map/all_to_all | solution.py:115
  76.0 1.3 compare_and_fusion
  77.3 13.9 %all-gather.2.cloned.1.call-done = bf16[2048,1024]{1,0:T(8,128)(2,1)} async-done(((bf16[2048,256]{1,0:T(8,128)(2,1)}), bf16[2048,1024]{1,0:T(8,128)(2,1)}) %all-gather.2.cloned.1.call-update) | async-done | bytes 4194320 | tf_op jit(solution)/shard_map/all_gather | solution.py:117
  91.3 3.2 %fusion.1 = f32[2048]{0:T(1024)S(1)} fusion(bf16[2048,1024]{1,0:T(8,128)(2,1)} %all-gather.2.cloned.1.call-done), kind=kLoop, calls=%fused_computation.5 | loop fusion | flops 6289408 | bytes 4202496 | tf_op jit(solution)/shard_map/reduce_sum | solution.py:36
  94.7 4.8 %convert_bitcast_fusion.2 = bf16[256,8,8,128]{3,1,2,0:T(8,128)(2,1)S(1)} fusion(bf16[1,1024,1024]{2,1,0:T(8,128)(2,1)S(1)} %copy-done, bf16[2048,1024]{1,0:T(8,128)(2,1)S(1)} %copy-done.2, f32[1024]{0:T(1024)S(1)} %bitcast.59, f32[2048]{0:T(1024)S(1)} %add_rsqrt_fusion), kind=kOutput, calls=%fused_computation.26 | convolution fusion | flops 4305453056 | bytes 10498048 | tf_op jit(solution)/shard_map/dot_general | solution.py:65
  99.6 1.1 copy.36
  100.7 0.4 copy-done.6
  101.2 4.8 %convert_bitcast_fusion.1 = bf16[256,8,8,128]{3,1,2,0:T(8,128)(2,1)S(1)} fusion(bf16[1,1024,1024]{2,1,0:T(8,128)(2,1)S(1)} %copy-done.6, bf16[2048,1024]{1,0:T(8,128)(2,1)S(1)} %copy-done.2, f32[1024]{0:T(1024)S(1)} %bitcast.60, f32[2048]{0:T(1024)S(1)} %add_rsqrt_fusion), kind=kOutput, calls=%fused_computation.25 | convolution fusion | flops 4305453056 | bytes 10498048 | tf_op jit(solution)/shard_map/dot_general | solution.py:68
  106.0 1.1 copy.37
  107.6 5.1 %convert_bitcast_fusion.3 = bf16[256,8,8,128]{3,1,2,0:T(8,128)(2,1)S(1)} fusion(bf16[1,1024,1024]{2,1,0:T(8,128)(2,1)S(1)} %copy-done.7, bf16[2048,1024]{1,0:T(8,128)(2,1)S(1)} %copy-done.2, f32[1024]{0:T(1024)S(1)} %bitcast.61, f32[2048]{0:T(1024)S(1)} %add_rsqrt_fusion), kind=kOutput, calls=%fused_computation.27 | convolution fusion | flops 4305453056 | bytes 10498048 | tf_op jit(solution)/shard_map/dot_general | solution.py:69
  112.7 3.0 %copy.35 = bf16[256,8,8,128]{3,2,1,0:T(8,128)(2,1)} copy(bf16[256,8,8,128]{3,1,2,0:T(8,128)(2,1)S(1)} %convert_bitcast_fusion.3) | data formatting | bytes 8388608
  115.7 3.0 %fusion.10 = f32[16,8,128,128]{2,3,1,0:T(8,128)S(1)} fusion(bf16[16,128,8,128]{3,2,1,0:T(8,128)(2,1)S(1)} %bitcast.49, bf16[16,128,8,128]{3,2,1,0:T(8,128)(2,1)S(1)} %bitcast.48), kind=kOutput, calls=%fused_computation.18 | convolution fusion | flops 536870912 | bytes 16777216 | tf_op jit(solution)/shard_map/bqhd,bkhd->bhqk/dot_general | solution.py:84
  118.7 4.3 %fusion.39 = (f32[16,8,128]{2,1,0:T(8,128)S(1)}, f32[16,8,128,128]{2,3,1,0:T(8,128)}) fusion(f32[16,8,128,128]{2,3,1,0:T(8,128)S(1)} %fusion.10, f32[8,128,128]{1,2,0:T(8,128)S(1)} %copy.30, pred[16,128,128]{1,2,0:T(8,128)(4,1)S(1)} %copy-done.3), kind=kOutput, calls=%fused_computation.58 | output fusion | flops 12583039 | bytes 17629184 | tf_op jit(solution)/shard_map/sub | solution.py:94
  123.0 8.2 %convert_bitcast_fusion = bf16[16,128,8,128]{1,3,2,0:T(8,128)(2,1)} fusion(f32[16,8,128,128]{2,3,1,0:T(8,128)} %get-tuple-element.6, f32[16,8,128]{2,1,0:T(8,128)S(1)} %get-tuple-element.5, bf16[16,128,8,128]{3,2,1,0:T(8,128)(2,1)} %bitcast.51), kind=kOutput, calls=%fused_computation.21 | convolution fusion | flops 543162368 | bytes 16842752 | tf_op jit(solution)/shard_map/bhqk,bkhd->bqhd/dot_general | solution.py:96
  131.3 6.9 %copy.33 = bf16[16,128,8,128]{3,2,1,0:T(8,128)(2,1)} copy(bf16[16,128,8,128]{1,3,2,0:T(8,128)(2,1)} %convert_bitcast_fusion) | data formatting | bytes 8388608 | tf_op jit(solution)/shard_map/convert_element_type | solution.py:99
  138.2 8.3 %fusion.17 = bf16[2048,1024]{1,0:T(8,128)(2,1)} fusion(bf16[256,8,8,128]{3,2,1,0:T(8,128)(2,1)} %bitcast.52, bf16[1,1024,1024]{2,1,0:T(8,128)(2,1)S(1)} %copy-done.8), kind=kOutput, calls=%fused_computation.29 | convolution fusion | flops 4297064448 | bytes 10485760 | tf_op jit(solution)/shard_map/dot_general | solution.py:129
  146.5 5.1 %all-to-all-start.2 = ((bf16[4,512,1024]{2,1,0:T(8,128)(2,1)}), bf16[4,512,1024]{2,1,0:T(8,128)(2,1)}, u32[]{:S(2)}, u32[]{:S(2)}) async-start(bf16[4,512,1024]{2,1,0:T(8,128)(2,1)} %bitcast.50), calls=%async_computation.2 | async-start | bytes 8388608 | tf_op jit(solution)/shard_map/all_to_all | solution.py:16
  151.6 0.5 broadcast.81
  152.1 0.7 reduce.5
  152.9 47.4 %all-to-all-done.2 = bf16[4,512,1024]{2,1,0:T(8,128)(2,1)} async-done(((bf16[4,512,1024]{2,1,0:T(8,128)(2,1)}), bf16[4,512,1024]{2,1,0:T(8,128)(2,1)}, u32[]{:S(2)}, u32[]{:S(2)}) %all-to-all-start.2) | async-done | bytes 4194336 | tf_op jit(solution)/shard_map/all_to_all | solution.py:16
  200.4 3.4 %convert_reduce_fusion = f32[512,1024]{1,0:T(8,128)S(1)} fusion(bf16[4,512,1024]{2,1,0:T(8,128)(2,1)} %all-to-all-done.2), kind=kLoop, calls=%fused_computation.8 | loop fusion | flops 3670016 | bytes 6291456 | tf_op jit(solution)/shard_map/reduce_sum | solution.py:17
  203.8 2.5 %select_convert_fusion = bf16[512,1024]{1,0:T(8,128)(2,1)} fusion(f32[512,1024]{1,0:T(8,128)S(1)} %convert_reduce_fusion, bf16[2048,1024]{1,0:T(8,128)(2,1)} %all-gather.2.cloned.1.call-done, s32[]{:T(128)S(6)} %select_n.49, pred[512]{0:T(512)(128)(4,1)S(1)} %dynamic-slice_compare_fusion), kind=kLoop, calls=%fused_computation.34 | loop fusion | flops 2097152 | bytes 4194820 | tf_op jit(solution)/shard_map/convert_element_type | solution.py:136
  (32 shorter events, 1.4 us)
Async XLA Ops:
  6.5 88.0 %copy-start = (bf16[1,1024,1024]{2,1,0:T(8,128)(2,1)S(1)}, bf16[1,1024,1024]{2,1,0:T(8,128)(2,1)}, u32[]{:S(2)}) copy-start(bf16[1,1024,1024]{2,1,0:T(8,128)(2,1)} %param.14) | copy-start | bytes 6291460
  6.5 62.5 %copy-start.4 = (s32[128,128]{1,0:T(8,128)S(1)}, s32[128,128]{1,0:T(8,128)}, u32[]{:S(2)}) copy-start(s32[128,128]{1,0:T(8,128)} %constant.44.clone) | copy-start | bytes 196612
  6.5 62.5 %copy-start.5 = (f32[1,32,8]{1,2,0:T(8,128)S(1)}, f32[1,32,8]{1,2,0:T(8,128)}, u32[]{:S(2)}) copy-start(f32[1,32,8]{1,2,0:T(8,128)} %param.18) | copy-start | bytes 3076
  6.5 84.7 %all-gather.2.cloned.1.call-start = ((), (), s32[]{:S(2)}) async-start(), calls=%async_computation.3 | async-start | bytes 5242880 | tf_op jit(solution)/shard_map/all_gather | solution.py:117
  52.3 42.2 %copy-start.9 = (f32[1,1024]{1,0:T(1,128)S(1)}, f32[1,1024]{1,0:T(1,128)}, u32[]{:S(2)}) copy-start(f32[1,1024]{1,0:T(1,128)} %param.13) | copy-start | bytes 12292
  65.0 10.9 %all-to-all-start = ((s32[32,1,64]{2,1,0:T(1,128)}), s32[32,1,64]{2,1,0:T(1,128)S(1)}, u32[]{:S(2)}, u32[]{:S(2)}) async-start(s32[32,1,64]{2,1,0:T(1,128)} %all_to_all.12), calls=%async_computation | async-start | bytes 32768 | tf_op jit(solution)/shard_map/all_to_all | solution.py:115
  91.3 3.4 %copy-start.2 = (bf16[2048,1024]{1,0:T(8,128)(2,1)S(1)}, bf16[2048,1024]{1,0:T(8,128)(2,1)}, u32[]{:S(2)}) copy-start(bf16[2048,1024]{1,0:T(8,128)(2,1)} %all-gather.2.cloned.1.call-done) | copy-start | bytes 12582916
  99.6 1.6 copy-start.6
  106.0 1.6 copy-start.7
  115.7 3.0 %copy-start.3 = (pred[16,128,128]{1,2,0:T(8,128)(4,1)S(1)}, pred[16,128,128]{1,2,0:T(8,128)(4,1)}, u32[]{:S(2)}) copy-start(pred[16,128,128]{1,2,0:T(8,128)(4,1)} %compare_and_fusion) | copy-start | bytes 786436
  131.3 6.9 %copy-start.8 = (bf16[1,1024,1024]{2,1,0:T(8,128)(2,1)S(1)}, bf16[1,1024,1024]{2,1,0:T(8,128)(2,1)}, u32[]{:S(2)}) copy-start(bf16[1,1024,1024]{2,1,0:T(8,128)(2,1)} %param.17) | copy-start | bytes 6291460
  146.5 53.9 %all-to-all-start.2 = ((bf16[4,512,1024]{2,1,0:T(8,128)(2,1)}), bf16[4,512,1024]{2,1,0:T(8,128)(2,1)}, u32[]{:S(2)}, u32[]{:S(2)}) async-start(bf16[4,512,1024]{2,1,0:T(8,128)(2,1)} %bitcast.50), calls=%async_computation.2 | async-start | bytes 8388608 | tf_op jit(solution)/shard_map/all_to_all | solution.py:16
  152.9 53.4 %copy-start.1 = (bf16[1,1024,1024]{2,1,0:T(8,128)(2,1)S(1)}, bf16[1,1024,1024]{2,1,0:T(8,128)(2,1)}, u32[]{:S(2)}) copy-start(bf16[1,1024,1024]{2,1,0:T(8,128)(2,1)} %param.14) | copy-start | bytes 6291460
Sparse Core Ops, SparseCore 0:
  52.5 38.7 all-gather.1
where the time goes:
time: 214 us; the launch traced here: 213 us
  waiting for transfers between devices  67.2 us (31%)
  local copies, waits for them, and re-layouts  43.8 us (20%)
  matrix products  35.1 us (16%)
  blocking collectives  26.3 us (12%)
  other arithmetic  18 us (8%)
  between operations  13.6 us (6%)
  starting transfers between devices  9.12 us (4%)
    all_to_all x1, waiting for transfers between devices, summed_on_arrival(): lax.all_to_all(in_blocks(value, dim, length), axis, 0, 0, tiled=True)  47.4 us
    all_to_all x1, blocking collectives, per_device(): lax.all_to_all(packed, 'tenant', split_axis=0, concat_axis=0, tiled=True)  26.3 us
    scatter x1, local copies, waits for them, and re-layouts, pack_rows(): packed = jnp.zeros((tenants * slot_rows, feature_count), tokens.dtype).at...  14.2 us
    all_gather x1, waiting for transfers between devices, per_device(): lax.all_gather(arrived.reshape(tenants * slot_rows, column_share), 'tp',...  13.9 us
    scatter x1, local copies, waits for them, and re-layouts, pack_rows(): jnp.full((tenants * slot_rows,), -1, jnp.int32).at[flat_target]  11.8 us
    dot_general x1, matrix products, per_device(): jnp.dot(context, out_weight, preferred_element_type=jnp.float32)  8.33 us
    dot_general x1, matrix products, attend(): jnp.einsum('bhqk,bkhd->bqhd', probabilities, value_blocks, preferred_elem...  8.23 us
    convert_element_type x1, local copies, waits for them, and re-layouts, attend(): context.astype(jnp.bfloat16).reshape(row_total, local_heads * head_size)  6.88 us
  transfers between devices with their start and end apart: 3, of which 3 were waited for; matrix products, arithmetic and copies ran while one was open for 7% of the time, Pallas kernels for 0%

commit v1 on v0

--- a/solution.py
+++ b/solution.py
@@ -114,9 +114,9 @@
         lax.all_to_all(packed, "tenant", split_axis=0, concat_axis=0, tiled=True),
         lax.all_to_all(segment, "tenant", split_axis=0, concat_axis=0, tiled=True),
     )
-    arrived = lax.all_gather(
-        arrived.reshape(tenants * slot_rows, column_share), "tp", axis=1, tiled=True
-    )
+    part = arrived.reshape(tenants * slot_rows, column_share)
+    sent = jnp.stack([part] * lax.axis_size("tp"))
+    arrived = jnp.concatenate(lax.all_to_all(sent, "tp", 0, 0), axis=1)
     arrived_segment = arrived_segment.reshape(-1)
     normed = rms_normed(arrived, norm_gain[0])
     context = attend(

time: 214 us -> 247 us (1.15)
  waiting for transfers between devices: 67.2 us -> 88.7 us
  starting transfers between devices: 9.12 us -> 22.7 us
  between operations: 13.6 us -> 0.22 us
  local copies, waits for them, and re-layouts: 43.8 us -> 56.3 us
    all_to_all x0 -> x1, waiting for transfers between devices: none -> 45.2 us  [per_device(): arrived = jnp.concatenate(lax.all_to_all(sent, 'tp', 0, 0), axis=1)]
    all_gather x1 -> x0, waiting for transfers between devices: 13.9 us -> none  [per_device(): lax.all_gather(arrived.reshape(tenants * slot_rows, column_share), 'tp',...]
    all_to_all x0 -> x1, starting transfers between devices: none -> 7.27 us  [per_device(): arrived = jnp.concatenate(lax.all_to_all(sent, 'tp', 0, 0), axis=1)]
    all_to_all x0 -> x1, local copies, waits for them, and re-layouts: none -> 6.27 us  [per_device(): arrived = jnp.concatenate(lax.all_to_all(sent, 'tp', 0, 0), axis=1)]
    all_to_all x1, waiting for transfers between devices: 5.86 us -> 0.01 us  [per_device(): lax.all_to_all(segment, 'tenant', split_axis=0, concat_axis=0, tiled=True)]
    all_to_all x1, starting transfers between devices: 4.05 us -> 9.71 us  [per_device(): lax.all_to_all(segment, 'tenant', split_axis=0, concat_axis=0, tiled=True)]
    all_to_all x1, waiting for transfers between devices: 47.4 us -> 43.5 us  [summed_on_arrival(): lax.all_to_all(in_blocks(value, dim, length), axis, 0, 0, tiled=True)]
    unnamed x23 -> x25, local copies, waits for them, and re-layouts: 6.39 us -> 8.07 us
  transfers between devices with their start and end apart: 3 -> 3, of which waited for: 3 -> 2; matrix products, arithmetic and copies ran while one was open for 7% -> 10% of each run, Pallas kernels for 0% -> 0%
where the time goes in v1:
time: 247 us; the launch traced here: 246 us
  waiting for transfers between devices  88.7 us (36%)
  local copies, waits for them, and re-layouts  56.3 us (23%)
  matrix products  35.4 us (14%)
  blocking collectives  24 us (10%)
  starting transfers between devices  22.7 us (9%)
  other arithmetic  18.4 us (7%)
    all_to_all x1, waiting for transfers between devices, per_device(): arrived = jnp.concatenate(lax.all_to_all(sent, 'tp', 0, 0), axis=1)  45.2 us
    all_to_all x1, waiting for transfers between devices, summed_on_arrival(): lax.all_to_all(in_blocks(value, dim, length), axis, 0, 0, tiled=True)  43.5 us
    all_to_all x1, blocking collectives, per_device(): lax.all_to_all(packed, 'tenant', split_axis=0, concat_axis=0, tiled=True)  24 us
    scatter x1, local copies, waits for them, and re-layouts, pack_rows(): packed = jnp.zeros((tenants * slot_rows, feature_count), tokens.dtype).at...  14.2 us
    scatter x1, local copies, waits for them, and re-layouts, pack_rows(): jnp.full((tenants * slot_rows,), -1, jnp.int32).at[flat_target]  11.8 us
    all_to_all x1, starting transfers between devices, per_device(): lax.all_to_all(segment, 'tenant', split_axis=0, concat_axis=0, tiled=True)  9.71 us
    dot_general x1, matrix products, per_device(): jnp.dot(context, out_weight, preferred_element_type=jnp.float32)  8.33 us
    dot_general x1, matrix products, attend(): jnp.einsum('bhqk,bkhd->bqhd', probabilities, value_blocks, preferred_elem...  8.23 us
  transfers between devices with their start and end apart: 3, of which 2 were waited for; matrix products, arithmetic and copies ran while one was open for 10% of the time, Pallas kernels for 0%

profile of v1, /device:TPU:1, one launch (start us, length us, event | category | flops | bytes accessed | tf_op | source)
XLA Modules:
  0.0 245.7 jit_solution(9393710693158774374)
XLA Ops:
  0.0 1.0 select_reduce_fusion
  1.7 0.7 add_select_fusion.4
  2.7 11.8 %scatter_custom_fusion = s32[2048]{0:T(1024)S(1)} fusion(s32[3072]{0:T(1024)S(1)} %bitcast.69, s32[3072]{0:T(1024)S(1)} %reshape.179, s32[]{:T(128)} %constant.18.clone.1), kind=kCustom, calls=%fused_computation.51 | custom fusion | bytes 8196 | tf_op jit(solution)/shard_map/scatter | solution.py:56
  15.2 9.7 %all-to-all-start = ((s32[32,1,64]{2,1,0:T(1,128)}), s32[32,1,64]{2,1,0:T(1,128)S(1)}, u32[]{:S(2)}, u32[]{:S(2)}) async-start(s32[32,1,64]{2,1,0:T(1,128)} %all_to_all.15), calls=%async_computation | async-start | bytes 32768 | tf_op jit(solution)/shard_map/all_to_all | solution.py:115
  24.9 2.7 %constant_dynamic-slice_fusion.1 = bf16[48,64,256]{2,1,0:T(8,128)(2,1)} fusion(bf16[48,64,1024]{2,1,0:T(8,128)(2,1)} %param.10, s32[]{:T(128)S(6)} %select_n.50), kind=kLoop, calls=%fused_computation.56 | loop fusion | bytes 3145732 | tf_op jit(solution)/shard_map/dynamic_slice | solution.py:109
  27.6 14.2 %scatter_custom_fusion.1 = bf16[2048,256]{1,0:T(8,128)(2,1)S(1)} fusion(s32[3072]{0:T(1024)S(1)} %bitcast.70, bf16[3072,256]{1,0:T(8,128)(2,1)} %bitcast.67, bf16[]{:T(256)} %constant.10.clone.1), kind=kCustom, calls=%fused_computation.40 | custom fusion | bytes 1049088 | tf_op jit(solution)/shard_map/scatter | solution.py:52
  41.8 24.0 %all_to_all.24 = bf16[32,64,256]{2,1,0:T(8,128)(2,1)S(1)} all-to-all(bf16[32,64,256]{2,1,0:T(8,128)(2,1)S(1)} %bitcast.66), channel_id=1, replica_groups=mesh['tenant'=32,'tp'=4] {'tenant'}, dimensions={0} | all-to-all | bytes 2097152 | tf_op jit(solution)/shard_map/all_to_all | solution.py:114
  65.8 2.2 stack.3
  68.1 7.3 %all-to-all-start.2 = ((bf16[4,2048,256]{2,1,0:T(8,128)(2,1)}), bf16[4,2048,256]{2,1,0:T(8,128)(2,1)}, u32[]{:S(2)}, u32[]{:S(2)}) async-start(bf16[4,2048,256]{2,1,0:T(8,128)(2,1)} %stack.3), calls=%async_computation.2 | async-start | bytes 8388608 | tf_op jit(solution)/shard_map/all_to_all | solution.py:119
  76.6 0.7 fusion.27
  77.6 1.4 compare_and_fusion
  79.0 45.2 %all-to-all-done.2 = bf16[4,2048,256]{2,1,0:T(8,128)(2,1)} async-done(((bf16[4,2048,256]{2,1,0:T(8,128)(2,1)}), bf16[4,2048,256]{2,1,0:T(8,128)(2,1)}, u32[]{:S(2)}, u32[]{:S(2)}) %all-to-all-start.2) | async-done | bytes 4194336 | tf_op jit(solution)/shard_map/all_to_all | solution.py:119
  124.1 6.3 %copy.44 = bf16[4,2048,256]{1,2,0:T(8,128)(2,1)} copy(bf16[4,2048,256]{2,1,0:T(8,128)(2,1)} %all-to-all-done.2) | data formatting | bytes 8388608 | tf_op jit(solution)/shard_map/all_to_all | solution.py:119
  130.4 3.2 %fusion.1 = f32[2048]{0:T(1024)S(1)} fusion(bf16[4,2048,256]{1,2,0:T(8,128)(2,1)} %copy.44), kind=kLoop, calls=%fused_computation.5 | loop fusion | flops 6289408 | bytes 4202496 | tf_op jit(solution)/shard_map/reduce_sum | solution.py:36
  133.8 1.0 fusion.3
  134.8 5.0 %convert_bitcast_fusion.1 = bf16[256,8,8,128]{3,1,2,0:T(8,128)(2,1)S(1)} fusion(bf16[2048,1024]{0,1:T(8,128)(2,1)S(1)} %bitcast.62, bf16[1,1024,1024]{2,1,0:T(8,128)(2,1)S(1)} %copy-done), kind=kOutput, calls=%fused_computation.25 | convolution fusion | flops 4297064448 | bytes 10485760 | tf_op jit(solution)/shard_map/dot_general | solution.py:68
  139.8 1.1 copy.56
  141.4 4.9 %convert_bitcast_fusion.2 = bf16[256,8,8,128]{3,1,2,0:T(8,128)(2,1)S(1)} fusion(bf16[2048,1024]{0,1:T(8,128)(2,1)S(1)} %bitcast.63, bf16[1,1024,1024]{2,1,0:T(8,128)(2,1)S(1)} %copy-done.7), kind=kOutput, calls=%fused_computation.26 | convolution fusion | flops 4297064448 | bytes 10485760 | tf_op jit(solution)/shard_map/dot_general | solution.py:65
  146.4 5.1 %convert_bitcast_fusion.3 = bf16[256,8,8,128]{3,1,2,0:T(8,128)(2,1)S(1)} fusion(bf16[2048,1024]{0,1:T(8,128)(2,1)S(1)} %bitcast.64, bf16[1,1024,1024]{2,1,0:T(8,128)(2,1)S(1)} %copy-done.8), kind=kOutput, calls=%fused_computation.27 | convolution fusion | flops 4297064448 | bytes 10485760 | tf_op jit(solution)/shard_map/dot_general | solution.py:69
  151.5 3.0 %copy.54 = bf16[256,8,8,128]{3,2,1,0:T(8,128)(2,1)} copy(bf16[256,8,8,128]{3,1,2,0:T(8,128)(2,1)S(1)} %convert_bitcast_fusion.3) | data formatting | bytes 8388608
  154.5 1.1 copy.55
  155.6 3.0 %fusion.10 = f32[16,8,128,128]{2,3,1,0:T(8,128)S(1)} fusion(bf16[16,128,8,128]{3,2,1,0:T(8,128)(2,1)S(1)} %bitcast.57, bf16[16,128,8,128]{3,2,1,0:T(8,128)(2,1)S(1)} %bitcast.58), kind=kOutput, calls=%fused_computation.18 | convolution fusion | flops 536870912 | bytes 16777216 | tf_op jit(solution)/shard_map/bqhd,bkhd->bhqk/dot_general | solution.py:84
  158.7 4.3 %fusion.36 = (f32[16,8,128]{2,1,0:T(8,128)S(1)}, f32[16,8,128,128]{2,3,1,0:T(8,128)}) fusion(f32[16,8,128,128]{2,3,1,0:T(8,128)S(1)} %fusion.10, f32[8,128,128]{1,2,0:T(8,128)S(1)} %copy.48, pred[16,128,128]{1,2,0:T(8,128)(4,1)S(1)} %copy-done.3), kind=kOutput, calls=%fused_computation.59 | output fusion | flops 12583039 | bytes 17629184 | tf_op jit(solution)/shard_map/sub | solution.py:94
  163.0 8.2 %convert_bitcast_fusion = bf16[16,128,8,128]{1,3,2,0:T(8,128)(2,1)} fusion(f32[16,8,128,128]{2,3,1,0:T(8,128)} %get-tuple-element.6, f32[16,8,128]{2,1,0:T(8,128)S(1)} %get-tuple-element.5, bf16[16,128,8,128]{3,2,1,0:T(8,128)(2,1)} %bitcast.61), kind=kOutput, calls=%fused_computation.21 | convolution fusion | flops 543162368 | bytes 16842752 | tf_op jit(solution)/shard_map/bhqk,bkhd->bqhd/dot_general | solution.py:96
  171.2 6.9 %copy.51 = bf16[16,128,8,128]{3,2,1,0:T(8,128)(2,1)} copy(bf16[16,128,8,128]{1,3,2,0:T(8,128)(2,1)} %convert_bitcast_fusion) | data formatting | bytes 8388608 | tf_op jit(solution)/shard_map/convert_element_type | solution.py:99
  178.1 8.3 %fusion.17 = bf16[2048,1024]{1,0:T(8,128)(2,1)} fusion(bf16[256,8,8,128]{3,2,1,0:T(8,128)(2,1)} %bitcast.65, bf16[1,1024,1024]{2,1,0:T(8,128)(2,1)S(1)} %copy-done.9), kind=kOutput, calls=%fused_computation.29 | convolution fusion | flops 4297064448 | bytes 10485760 | tf_op jit(solution)/shard_map/dot_general | solution.py:129
  186.4 5.8 %all-to-all-start.3 = ((bf16[4,512,1024]{2,1,0:T(8,128)(2,1)}), bf16[4,512,1024]{2,1,0:T(8,128)(2,1)}, u32[]{:S(2)}, u32[]{:S(2)}) async-start(bf16[4,512,1024]{2,1,0:T(8,128)(2,1)} %bitcast.60), calls=%async_computation.3 | async-start | bytes 8388608 | tf_op jit(solution)/shard_map/all_to_all | solution.py:16
  193.6 2.3 constant_dynamic-slice_fusion
  195.8 1.6 copy.53
  197.5 43.5 %all-to-all-done.3 = bf16[4,512,1024]{2,1,0:T(8,128)(2,1)} async-done(((bf16[4,512,1024]{2,1,0:T(8,128)(2,1)}), bf16[4,512,1024]{2,1,0:T(8,128)(2,1)}, u32[]{:S(2)}, u32[]{:S(2)}) %all-to-all-start.3) | async-done | bytes 4194336 | tf_op jit(solution)/shard_map/all_to_all | solution.py:16
  241.0 3.4 %convert_reduce_fusion = f32[512,1024]{1,0:T(8,128)S(1)} fusion(bf16[4,512,1024]{2,1,0:T(8,128)(2,1)} %all-to-all-done.3), kind=kLoop, calls=%fused_computation.8 | loop fusion | flops 3670016 | bytes 6291456 | tf_op jit(solution)/shard_map/reduce_sum | solution.py:17
  244.4 1.3 select_convert_fusion
  (39 shorter events, 5.1 us)
Async XLA Ops:
  0.0 134.8 %copy-start = (bf16[1,1024,1024]{2,1,0:T(8,128)(2,1)S(1)}, bf16[1,1024,1024]{2,1,0:T(8,128)(2,1)}, u32[]{:S(2)}) copy-start(bf16[1,1024,1024]{2,1,0:T(8,128)(2,1)} %param.15) | copy-start | bytes 6291460
  15.2 26.7 %all-to-all-start = ((s32[32,1,64]{2,1,0:T(1,128)}), s32[32,1,64]{2,1,0:T(1,128)S(1)}, u32[]{:S(2)}, u32[]{:S(2)}) async-start(s32[32,1,64]{2,1,0:T(1,128)} %all_to_all.15), calls=%async_computation | async-start | bytes 32768 | tf_op jit(solution)/shard_map/all_to_all | solution.py:115
  68.1 7.8 %copy-start.6 = (f32[1,1024]{1,0:T(1,128)S(1)}, f32[1,1024]{1,0:T(1,128)}, u32[]{:S(2)}) copy-start(f32[1,1024]{1,0:T(1,128)} %param.13) | copy-start | bytes 12292
  68.1 8.5 %copy-start.4 = (s32[128,128]{1,0:T(8,128)S(1)}, s32[128,128]{1,0:T(8,128)}, u32[]{:S(2)}) copy-start(s32[128,128]{1,0:T(8,128)} %constant.44.clone) | copy-start | bytes 196612
  68.1 8.5 %copy-start.5 = (f32[1,32,8]{1,2,0:T(8,128)S(1)}, f32[1,32,8]{1,2,0:T(8,128)}, u32[]{:S(2)}) copy-start(f32[1,32,8]{1,2,0:T(8,128)} %param.18) | copy-start | bytes 3076
  68.1 56.1 %all-to-all-start.2 = ((bf16[4,2048,256]{2,1,0:T(8,128)(2,1)}), bf16[4,2048,256]{2,1,0:T(8,128)(2,1)}, u32[]{:S(2)}, u32[]{:S(2)}) async-start(bf16[4,2048,256]{2,1,0:T(8,128)(2,1)} %stack.3), calls=%async_computation.2 | async-start | bytes 8388608 | tf_op jit(solution)/shard_map/all_to_all | solution.py:119
  130.4 3.4 %copy-start.2 = (bf16[4,2048,256]{1,2,0:T(8,128)(2,1)S(1)}, bf16[4,2048,256]{1,2,0:T(8,128)(2,1)}, u32[]{:S(2)}) copy-start(bf16[4,2048,256]{1,2,0:T(8,128)(2,1)} %copy.44) | copy-start | bytes 12582916
  139.8 1.6 copy-start.7
  141.4 5.0 %copy-start.8 = (bf16[1,1024,1024]{2,1,0:T(8,128)(2,1)S(1)}, bf16[1,1024,1024]{2,1,0:T(8,128)(2,1)}, u32[]{:S(2)}) copy-start(bf16[1,1024,1024]{2,1,0:T(8,128)(2,1)} %param.16) | copy-start | bytes 6291460
  155.6 3.1 %copy-start.3 = (pred[16,128,128]{1,2,0:T(8,128)(4,1)S(1)}, pred[16,128,128]{1,2,0:T(8,128)(4,1)}, u32[]{:S(2)}) copy-start(pred[16,128,128]{1,2,0:T(8,128)(4,1)} %compare_and_fusion) | copy-start | bytes 786436
  171.2 6.9 %copy-start.9 = (bf16[1,1024,1024]{2,1,0:T(8,128)(2,1)S(1)}, bf16[1,1024,1024]{2,1,0:T(8,128)(2,1)}, u32[]{:S(2)}) copy-start(bf16[1,1024,1024]{2,1,0:T(8,128)(2,1)} %param.17) | copy-start | bytes 6291460
  186.4 54.6 %all-to-all-start.3 = ((bf16[4,512,1024]{2,1,0:T(8,128)(2,1)}), bf16[4,512,1024]{2,1,0:T(8,128)(2,1)}, u32[]{:S(2)}, u32[]{:S(2)}) async-start(bf16[4,512,1024]{2,1,0:T(8,128)(2,1)} %bitcast.60), calls=%async_computation.3 | async-start | bytes 8388608 | tf_op jit(solution)/shard_map/all_to_all | solution.py:16
  195.8 49.9 %copy-start.1 = (bf16[1,1024,1024]{2,1,0:T(8,128)(2,1)S(1)}, bf16[1,1024,1024]{2,1,0:T(8,128)(2,1)}, u32[]{:S(2)}) copy-start(bf16[1,1024,1024]{2,1,0:T(8,128)(2,1)} %param.15) | copy-start | bytes 6291460
